TPU v7x, 32 devices: a whole 2x2x4 slice. The times are simulated.
32 devices in a mesh: scen: 2 (over y), cell: 4 (over z), obs: 4 (over x, core).
Axes of the slice: x: 2, y: 2, z: 4, core: 2. Of those that a mesh axis runs over, the one named last changes fastest.
Arguments:
- prior: bfloat16 [400, 2048], P('scen', 'cell'), parts along dimension 0, may hold values from -6 to 6
- obs_block: int32 [4096], P('obs'), may hold values from 0 to 15
- obs_weight: bfloat16 [4096, 128], P('obs'), may hold values from -0.5 to 0.5
- observed: float32 [8192], P(('scen', 'obs')), parts along dimension 0, may hold values from -8 to 8
- obs_sigma: float32 [4096], P('obs'), may hold values from 0.5 to 1.5
- pert_seed: int32 [6, 200, 4096], P('scen', None, 'obs'), parts along dimension 0, may hold values from 0 to 1048575
Outputs:
- posterior: bfloat16 [400, 2048], P('scen', 'cell'), parts along dimension 0
- post_predicted: float32 [400, 4096], P('scen', 'obs'), parts along dimension 0
There are 2 independent parts, one for each index of `scen`. A program takes and returns all parts, laid end to end along the dimension named above; an argument that names none is the same for every part. Nothing has to cross between parts.
All inputs are finite; a program needn't handle non-finite values.
Results may differ from a plain program's by a relative error of at most 0.0013.
Values sent between devices are 32-bit elements; how exact they have to be, the bound alone decides.
A program may use at most 64 MiB of HBM per device.

v0:
```python
import jax
import jax.numpy as jnp
from jax import lax
from jax.sharding import PartitionSpec as P

BLK = 128
ITERS = 3


def local_partial(param_field, local_index, weights):
    members = param_field.shape[0]
    nblocks = param_field.shape[1] // BLK
    blocks = param_field.reshape(members, nblocks, BLK)
    obs_count = local_index.shape[0]
    groups = obs_count // 64
    indices = local_index.reshape(groups, 64)
    group_weights = weights.reshape(groups, 64, BLK)

    def one_group(operands):
        group_index, group_weight = operands
        picked = jnp.take(blocks, group_index, axis=1)
        return jnp.sum(picked * group_weight[None], axis=2)

    result = lax.map(one_group, (indices, group_weights))
    return jnp.transpose(result, (1, 0, 2)).reshape(members, obs_count)


def per_device(prior, obs_block, obs_weight, observed, obs_sigma, pert_seed):
    members = prior.shape[0]
    nblocks = prior.shape[1] // BLK
    hp = lax.Precision.HIGHEST
    first_block = lax.axis_index("cell") * nblocks
    local_block = obs_block - first_block
    inside = jnp.logical_and(local_block >= 0, local_block < nblocks)
    clipped = jnp.clip(local_block, 0, nblocks - 1)
    weights = obs_weight.astype(jnp.float32) * inside[:, None].astype(jnp.float32)
    param_field = prior.astype(jnp.float32)
    inflation = jnp.float32(ITERS)
    root_scale = jnp.sqrt(jnp.float32(members - 1.0))
    identity = jnp.eye(members, dtype=jnp.float32)
    partial_terms = local_partial(param_field, clipped, weights)
    predicted = lax.psum(partial_terms, "cell")
    for step_index in range(ITERS):
        noise = jnp.sqrt(jnp.float32(3.0)) * (
            (2.0 * pert_seed[step_index].astype(jnp.float32) + 1.0) / 1048576.0 - 1.0
        )
        misfit = observed[None, :] + jnp.sqrt(inflation) * obs_sigma[None, :] * noise - predicted
        dev_pred = predicted - jnp.mean(predicted, axis=0, keepdims=True)
        dev_field = param_field - jnp.mean(param_field, axis=0, keepdims=True)
        scaled_dev = dev_pred / (obs_sigma[None, :] * root_scale)
        scaled_misfit = misfit / obs_sigma[None, :]
        gram_matrix = jnp.dot(scaled_dev, scaled_dev.T, precision=hp)
        cross_term = jnp.dot(scaled_dev, scaled_misfit.T, precision=hp)
        gram_matrix, cross_term = lax.psum((gram_matrix, cross_term), "obs")
        factor = jnp.linalg.cholesky(gram_matrix + inflation * identity)
        member_weight = jax.scipy.linalg.cho_solve((factor, True), cross_term)
        param_field = param_field + jnp.dot(member_weight.T, dev_field, precision=hp) / root_scale
        predicted = predicted + jnp.dot(member_weight.T, dev_pred, precision=hp) / root_scale
    return (param_field.astype(jnp.bfloat16), predicted)


def solution(mesh):
    return jax.shard_map(
        per_device,
        mesh=mesh,
        in_specs=(
            P("scen", "cell"),
            P("obs"),
            P("obs", None),
            P(("scen", "obs")),
            P("obs"),
            P("scen", None, "obs"),
        ),
        out_specs=(P("scen", "cell"), P("scen", "obs")),
        check_vma=False,
    )
```

profile of v0, /device:TPU:0, one launch (start us, length us, event | category | flops | bytes accessed | tf_op | source)
XLA Modules:
  0.0 502.5 jit_solution(17134970231463933520)
XLA Ops:
  10.8 143.9 %while.14 = (s32[]{:T(128)}, f32[16,200,64]{1,2,0:T(8,128)S(1)}, s32[16,64]{1,0:T(8,128)S(1)}, f32[200,4,128]{2,0,1:T(8,128)S(1)}, f32[16,64,128]{2,1,0:T(8,128)S(1)}, /*index=5*/s32[]{:T(128)}) while((s32[]{:T(128)}, f32[16,200,64]{1,2,0:T(8,128)S(1)}, s32[16,64]{1,0:T(8,128)S(1)}, f32[200,4,128]{2,0,1:T(8,128)S(1)}, ...), condition=%wide.region_2.3_spmd, body=%wide.region_0.2_spmd.sunk | while | flops 4904002 | bytes 19946964 | solution.py:24
  14.6 5.2 %multiply_reduce_fusion.2 = f32[64,200]{1,0:T(8,128)S(1)} fusion(f32[64,200,128]{2,1,0:T(8,128)} %gather_fusion, f32[64,128]{1,0:T(8,128)S(1)} %dynamic-slice_bitcast_fusion.2, pred[64]{0:T(512)(128)(4,1)S(1)} %compare_and_fusion.2), kind=kLoop, calls=%fused_computation.1.clone.1 | loop fusion | flops 4902400 | bytes 6637632 | tf_op jit(solution)/shard_map/while/body/eval_jaxpr/reduce_sum | solution.py:22
  23.6 5.2 %multiply_reduce_fusion.2 = f32[64,200]{1,0:T(8,128)S(1)} fusion(f32[64,200,128]{2,1,0:T(8,128)} %gather_fusion, f32[64,128]{1,0:T(8,128)S(1)} %dynamic-slice_bitcast_fusion.2, pred[64]{0:T(512)(128)(4,1)S(1)} %compare_and_fusion.2), kind=kLoop, calls=%fused_computation.1.clone.1 | loop fusion | flops 4902400 | bytes 6637632 | tf_op jit(solution)/shard_map/while/body/eval_jaxpr/reduce_sum | solution.py:22
  32.6 5.2 %multiply_reduce_fusion.2 = f32[64,200]{1,0:T(8,128)S(1)} fusion(f32[64,200,128]{2,1,0:T(8,128)} %gather_fusion, f32[64,128]{1,0:T(8,128)S(1)} %dynamic-slice_bitcast_fusion.2, pred[64]{0:T(512)(128)(4,1)S(1)} %compare_and_fusion.2), kind=kLoop, calls=%fused_computation.1.clone.1 | loop fusion | flops 4902400 | bytes 6637632 | tf_op jit(solution)/shard_map/while/body/eval_jaxpr/reduce_sum | solution.py:22
  41.6 5.2 %multiply_reduce_fusion.2 = f32[64,200]{1,0:T(8,128)S(1)} fusion(f32[64,200,128]{2,1,0:T(8,128)} %gather_fusion, f32[64,128]{1,0:T(8,128)S(1)} %dynamic-slice_bitcast_fusion.2, pred[64]{0:T(512)(128)(4,1)S(1)} %compare_and_fusion.2), kind=kLoop, calls=%fused_computation.1.clone.1 | loop fusion | flops 4902400 | bytes 6637632 | tf_op jit(solution)/shard_map/while/body/eval_jaxpr/reduce_sum | solution.py:22
  50.6 5.2 %multiply_reduce_fusion.2 = f32[64,200]{1,0:T(8,128)S(1)} fusion(f32[64,200,128]{2,1,0:T(8,128)} %gather_fusion, f32[64,128]{1,0:T(8,128)S(1)} %dynamic-slice_bitcast_fusion.2, pred[64]{0:T(512)(128)(4,1)S(1)} %compare_and_fusion.2), kind=kLoop, calls=%fused_computation.1.clone.1 | loop fusion | flops 4902400 | bytes 6637632 | tf_op jit(solution)/shard_map/while/body/eval_jaxpr/reduce_sum | solution.py:22
  59.5 5.2 %multiply_reduce_fusion.2 = f32[64,200]{1,0:T(8,128)S(1)} fusion(f32[64,200,128]{2,1,0:T(8,128)} %gather_fusion, f32[64,128]{1,0:T(8,128)S(1)} %dynamic-slice_bitcast_fusion.2, pred[64]{0:T(512)(128)(4,1)S(1)} %compare_and_fusion.2), kind=kLoop, calls=%fused_computation.1.clone.1 | loop fusion | flops 4902400 | bytes 6637632 | tf_op jit(solution)/shard_map/while/body/eval_jaxpr/reduce_sum | solution.py:22
  68.5 5.2 %multiply_reduce_fusion.2 = f32[64,200]{1,0:T(8,128)S(1)} fusion(f32[64,200,128]{2,1,0:T(8,128)} %gather_fusion, f32[64,128]{1,0:T(8,128)S(1)} %dynamic-slice_bitcast_fusion.2, pred[64]{0:T(512)(128)(4,1)S(1)} %compare_and_fusion.2), kind=kLoop, calls=%fused_computation.1.clone.1 | loop fusion | flops 4902400 | bytes 6637632 | tf_op jit(solution)/shard_map/while/body/eval_jaxpr/reduce_sum | solution.py:22
  77.5 5.2 %multiply_reduce_fusion.2 = f32[64,200]{1,0:T(8,128)S(1)} fusion(f32[64,200,128]{2,1,0:T(8,128)} %gather_fusion, f32[64,128]{1,0:T(8,128)S(1)} %dynamic-slice_bitcast_fusion.2, pred[64]{0:T(512)(128)(4,1)S(1)} %compare_and_fusion.2), kind=kLoop, calls=%fused_computation.1.clone.1 | loop fusion | flops 4902400 | bytes 6637632 | tf_op jit(solution)/shard_map/while/body/eval_jaxpr/reduce_sum | solution.py:22
  86.5 5.2 %multiply_reduce_fusion.2 = f32[64,200]{1,0:T(8,128)S(1)} fusion(f32[64,200,128]{2,1,0:T(8,128)} %gather_fusion, f32[64,128]{1,0:T(8,128)S(1)} %dynamic-slice_bitcast_fusion.2, pred[64]{0:T(512)(128)(4,1)S(1)} %compare_and_fusion.2), kind=kLoop, calls=%fused_computation.1.clone.1 | loop fusion | flops 4902400 | bytes 6637632 | tf_op jit(solution)/shard_map/while/body/eval_jaxpr/reduce_sum | solution.py:22
  95.5 5.2 %multiply_reduce_fusion.2 = f32[64,200]{1,0:T(8,128)S(1)} fusion(f32[64,200,128]{2,1,0:T(8,128)} %gather_fusion, f32[64,128]{1,0:T(8,128)S(1)} %dynamic-slice_bitcast_fusion.2, pred[64]{0:T(512)(128)(4,1)S(1)} %compare_and_fusion.2), kind=kLoop, calls=%fused_computation.1.clone.1 | loop fusion | flops 4902400 | bytes 6637632 | tf_op jit(solution)/shard_map/while/body/eval_jaxpr/reduce_sum | solution.py:22
  104.5 5.2 %multiply_reduce_fusion.2 = f32[64,200]{1,0:T(8,128)S(1)} fusion(f32[64,200,128]{2,1,0:T(8,128)} %gather_fusion, f32[64,128]{1,0:T(8,128)S(1)} %dynamic-slice_bitcast_fusion.2, pred[64]{0:T(512)(128)(4,1)S(1)} %compare_and_fusion.2), kind=kLoop, calls=%fused_computation.1.clone.1 | loop fusion | flops 4902400 | bytes 6637632 | tf_op jit(solution)/shard_map/while/body/eval_jaxpr/reduce_sum | solution.py:22
  113.5 5.2 %multiply_reduce_fusion.2 = f32[64,200]{1,0:T(8,128)S(1)} fusion(f32[64,200,128]{2,1,0:T(8,128)} %gather_fusion, f32[64,128]{1,0:T(8,128)S(1)} %dynamic-slice_bitcast_fusion.2, pred[64]{0:T(512)(128)(4,1)S(1)} %compare_and_fusion.2), kind=kLoop, calls=%fused_computation.1.clone.1 | loop fusion | flops 4902400 | bytes 6637632 | tf_op jit(solution)/shard_map/while/body/eval_jaxpr/reduce_sum | solution.py:22
  122.5 5.2 %multiply_reduce_fusion.2 = f32[64,200]{1,0:T(8,128)S(1)} fusion(f32[64,200,128]{2,1,0:T(8,128)} %gather_fusion, f32[64,128]{1,0:T(8,128)S(1)} %dynamic-slice_bitcast_fusion.2, pred[64]{0:T(512)(128)(4,1)S(1)} %compare_and_fusion.2), kind=kLoop, calls=%fused_computation.1.clone.1 | loop fusion | flops 4902400 | bytes 6637632 | tf_op jit(solution)/shard_map/while/body/eval_jaxpr/reduce_sum | solution.py:22
  131.5 5.2 %multiply_reduce_fusion.2 = f32[64,200]{1,0:T(8,128)S(1)} fusion(f32[64,200,128]{2,1,0:T(8,128)} %gather_fusion, f32[64,128]{1,0:T(8,128)S(1)} %dynamic-slice_bitcast_fusion.2, pred[64]{0:T(512)(128)(4,1)S(1)} %compare_and_fusion.2), kind=kLoop, calls=%fused_computation.1.clone.1 | loop fusion | flops 4902400 | bytes 6637632 | tf_op jit(solution)/shard_map/while/body/eval_jaxpr/reduce_sum | solution.py:22
  140.5 5.2 %multiply_reduce_fusion.2 = f32[64,200]{1,0:T(8,128)S(1)} fusion(f32[64,200,128]{2,1,0:T(8,128)} %gather_fusion, f32[64,128]{1,0:T(8,128)S(1)} %dynamic-slice_bitcast_fusion.2, pred[64]{0:T(512)(128)(4,1)S(1)} %compare_and_fusion.2), kind=kLoop, calls=%fused_computation.1.clone.1 | loop fusion | flops 4902400 | bytes 6637632 | tf_op jit(solution)/shard_map/while/body/eval_jaxpr/reduce_sum | solution.py:22
  156.1 47.5 %all-reduce.11.cloned.1.call-done = f32[200,1024]{1,0:T(8,128)} async-done(((f32[200,1024]{1,0:T(8,128)}), f32[200,1024]{1,0:T(8,128)}) %all-reduce.11.cloned.1.call-update) | async-done | bytes 819216 | tf_op jit(solution)/shard_map/psum | solution.py:42
  211.9 31.2 %all-reduce.17.cloned.1.call-done = (f32[200,200]{1,0:T(8,128)}, f32[200,200]{0,1:T(8,128)}) async-done(((f32[200,200]{1,0:T(8,128)}, f32[200,200]{0,1:T(8,128)}), (f32[200,200]{1,0:T(8,128)}, f32[200,200]{0,1:T(8,128)})) %all-reduce.17.cloned.1.call-update) | async-done | bytes 320016 | tf_op jit(solution)/shard_map/psum | solution.py:54
  245.2 11.7 %cholesky.182 = f32[128,128]{1,0:T(8,128)S(1)} custom-call(f32[128,128]{1,0:T(8,128)S(1)} %cholesky.292), custom_call_target="Cholesky" | custom-call | tf_op jit(solution)/shard_map/jit(cholesky)/cholesky | solution.py:55
  257.0 9.8 %custom-call.17 = f32[1,128,128]{1,2,0:T(8,128)S(1)} custom-call(f32[1,128,128]{2,1,0:T(8,128)S(1)} %get-tuple-element.95), custom_call_target="InvertDiagBlocksLowerTriangular" | custom-call | tf_op jit(solution)/shard_map/jit(cholesky)/cholesky | solution.py:55
  267.2 6.6 %cholesky.202 = f32[72,72]{1,0:T(8,128)S(1)} custom-call(f32[72,72]{1,0:T(8,128)S(1)} %convolution_subtract_fusion.8), custom_call_target="Cholesky" | custom-call | tf_op jit(solution)/shard_map/jit(cholesky)/cholesky | solution.py:55
  276.6 19.8 %custom-call.18 = f32[2,128,128]{1,2,0:T(8,128)S(1)} custom-call(f32[2,128,128]{2,1,0:T(8,128)S(1)} %pad_maximum_fusion.9), custom_call_target="InvertDiagBlocksLowerTriangular" | custom-call | tf_op jit(solution)/shard_map/jit(_cho_solve)/triangular_solve | solution.py:56
  306.6 32.8 %all-reduce.15.cloned.1.call-done = (f32[200,200]{1,0:T(8,128)}, f32[200,200]{0,1:T(8,128)}) async-done(((f32[200,200]{1,0:T(8,128)}, f32[200,200]{0,1:T(8,128)}), (f32[200,200]{1,0:T(8,128)}, f32[200,200]{0,1:T(8,128)})) %all-reduce.15.cloned.1.call-update) | async-done | bytes 320016 | tf_op jit(solution)/shard_map/psum | solution.py:54
  341.5 11.7 %cholesky.220 = f32[128,128]{1,0:T(8,128)S(1)} custom-call(f32[128,128]{1,0:T(8,128)S(1)} %cholesky.295), custom_call_target="Cholesky" | custom-call | tf_op jit(solution)/shard_map/jit(cholesky)/cholesky | solution.py:55
  353.3 9.8 %custom-call.19 = f32[1,128,128]{1,2,0:T(8,128)S(1)} custom-call(f32[1,128,128]{2,1,0:T(8,128)S(1)} %get-tuple-element.93), custom_call_target="InvertDiagBlocksLowerTriangular" | custom-call | tf_op jit(solution)/shard_map/jit(cholesky)/cholesky | solution.py:55
  363.5 6.6 %cholesky.240 = f32[72,72]{1,0:T(8,128)S(1)} custom-call(f32[72,72]{1,0:T(8,128)S(1)} %convolution_subtract_fusion.7), custom_call_target="Cholesky" | custom-call | tf_op jit(solution)/shard_map/jit(cholesky)/cholesky | solution.py:55
  372.9 19.9 %custom-call.20 = f32[2,128,128]{1,2,0:T(8,128)S(1)} custom-call(f32[2,128,128]{2,1,0:T(8,128)S(1)} %pad_maximum_fusion.10), custom_call_target="InvertDiagBlocksLowerTriangular" | custom-call | tf_op jit(solution)/shard_map/jit(_cho_solve)/triangular_solve | solution.py:56
  402.8 32.5 %all-reduce.13.cloned.1.call-done = (f32[200,200]{1,0:T(8,128)}, f32[200,200]{0,1:T(8,128)}) async-done(((f32[200,200]{1,0:T(8,128)}, f32[200,200]{0,1:T(8,128)}), (f32[200,200]{1,0:T(8,128)}, f32[200,200]{0,1:T(8,128)})) %all-reduce.13.cloned.1.call-update) | async-done | bytes 320016 | tf_op jit(solution)/shard_map/psum | solution.py:54
  437.3 11.7 %cholesky.258 = f32[128,128]{1,0:T(8,128)S(1)} custom-call(f32[128,128]{1,0:T(8,128)S(1)} %cholesky.298), custom_call_target="Cholesky" | custom-call | tf_op jit(solution)/shard_map/jit(cholesky)/cholesky | solution.py:55
  449.1 9.8 %custom-call.21 = f32[1,128,128]{1,2,0:T(8,128)S(1)} custom-call(f32[1,128,128]{2,1,0:T(8,128)S(1)} %get-tuple-element.91), custom_call_target="InvertDiagBlocksLowerTriangular" | custom-call | tf_op jit(solution)/shard_map/jit(cholesky)/cholesky | solution.py:55
  459.4 6.8 %cholesky.278 = f32[72,72]{1,0:T(8,128)S(1)} custom-call(f32[72,72]{1,0:T(8,128)S(1)} %convolution_subtract_fusion.6), custom_call_target="Cholesky" | custom-call | tf_op jit(solution)/shard_map/jit(cholesky)/cholesky | solution.py:55
  469.0 19.7 %custom-call.22 = f32[2,128,128]{1,2,0:T(8,128)S(1)} custom-call(f32[2,128,128]{2,1,0:T(8,128)S(1)} %pad_maximum_fusion.11), custom_call_target="InvertDiagBlocksLowerTriangular" | custom-call | tf_op jit(solution)/shard_map/jit(_cho_solve)/triangular_solve | solution.py:56
  (211 shorter events, 117.1 us)
Async XLA Ops:
  7.2 196.4 %all-reduce.11.cloned.1.call-start = ((), (), s32[]{:S(2)}) async-start(), calls=%async_computation | async-start | bytes 1638400 | tf_op jit(solution)/shard_map/psum | solution.py:42
  10.8 145.2 %copy-start.1 = (bf16[200,512]{1,0:T(8,128)(2,1)S(1)}, bf16[200,512]{1,0:T(8,128)(2,1)}, u32[]{:S(2)}) copy-start(bf16[200,512]{1,0:T(8,128)(2,1)} %param.11) | copy-start | bytes 614404
  10.8 145.3 %copy-start.2 = (f32[1024]{0:T(1024)S(1)}, f32[1024]{0:T(1024)}, u32[]{:S(2)}) copy-start(f32[1024]{0:T(1024)} %param.15) | copy-start | bytes 12292
  154.7 53.1 %copy-start.3 = (f32[1024]{0:T(1024)S(1)}, f32[1024]{0:T(1024)}, u32[]{:S(2)}) copy-start(f32[1024]{0:T(1024)} %param.14) | copy-start | bytes 12292
  155.9 87.2 %all-reduce.17.cloned.1.call-start = ((), (), s32[]{:S(2)}) async-start(), calls=%async_computation.3 | async-start | bytes 819200 | tf_op jit(solution)/shard_map/psum | solution.py:54
  207.8 92.5 %copy-start = (f32[200,1024]{1,0:T(8,128)S(1)}, f32[200,1024]{1,0:T(8,128)}, u32[]{:S(2)}) copy-start(f32[200,1024]{1,0:T(8,128)} %all-reduce.11.cloned.1.call-done) | copy-start | bytes 2457604
  211.3 128.2 %all-reduce.15.cloned.1.call-start = ((), (), s32[]{:S(2)}) async-start(), calls=%async_computation.2 | async-start | bytes 819200 | tf_op jit(solution)/shard_map/psum | solution.py:54
  306.4 128.9 %all-reduce.13.cloned.1.call-start = ((), (), s32[]{:S(2)}) async-start(), calls=%async_computation.1 | async-start | bytes 819200 | tf_op jit(solution)/shard_map/psum | solution.py:54
Sparse Core Ops, SparseCore 0:
  156.1 47.4 all-reduce.10
  211.4 31.6 all-reduce.16
  306.5 32.9 all-reduce.14
  402.3 32.9 all-reduce.12
where the time goes:
time: 508 us; the launch traced here: 503 us
  other arithmetic  242 us (48%)
  waiting for transfers between devices  144 us (28%)
  local copies, waits for them, and re-layouts  61.6 us (12%)
  matrix products  33.9 us (7%)
  between operations  18.7 us (4%)
    psum x3, waiting for transfers between devices, per_device(): gram_matrix, cross_term = lax.psum((gram_matrix, cross_term), 'obs')  96.6 us
    another operation x21, other arithmetic, per_device(): factor = jnp.linalg.cholesky(gram_matrix + inflation * identity)  88.6 us
    reduce_sum x16, other arithmetic, one_group(): return jnp.sum(picked * group_weight[None], axis=2)  83 us
    another operation x14, other arithmetic, per_device(): member_weight = jax.scipy.linalg.cho_solve((factor, True), cross_term)  59.8 us
    gather x16, local copies, waits for them, and re-layouts, one_group(): picked = jnp.take(blocks, group_index, axis=1)  59.3 us
    psum x1, waiting for transfers between devices, per_device(): predicted = lax.psum(partial_terms, 'cell')  47.5 us
    another operation x18, matrix products, per_device(): member_weight = jax.scipy.linalg.cho_solve((factor, True), cross_term)  11.1 us
  transfers between devices with their start and end apart: 4, of which 4 were waited for; matrix products, arithmetic and copies ran while one was open for 0% of the time, Pallas kernels for 0%

commit v1 on v0

--- a/solution.py
+++ b/solution.py
@@ -39,7 +39,11 @@
     root_scale = jnp.sqrt(jnp.float32(members - 1.0))
     identity = jnp.eye(members, dtype=jnp.float32)
     partial_terms = local_partial(param_field, clipped, weights)
-    predicted = lax.psum(partial_terms, "cell")
+    predicted = partial_terms
+    for hop in (1, 2):
+        predicted = predicted + lax.ppermute(
+            predicted, "cell", [(dev, dev ^ hop) for dev in range(4)]
+        )
     for step_index in range(ITERS):
         noise = jnp.sqrt(jnp.float32(3.0)) * (
             (2.0 * pert_seed[step_index].astype(jnp.float32) + 1.0) / 1048576.0 - 1.0

time: 508 us -> 518 us (1.020)
  waiting for transfers between devices: 144 us -> 152 us
  starting transfers between devices: 0.9 us -> 6.84 us
    ppermute x0 -> x2, waiting for transfers between devices: none -> 53.3 us  [per_device(): lax.ppermute(predicted, 'cell', [(dev, dev ^ hop) for dev in range(4)])]
    psum x1 -> x0, waiting for transfers between devices: 47.5 us -> none  [per_device(): predicted = lax.psum(partial_terms, 'cell')]
    ppermute x0 -> x2, starting transfers between devices: none -> 5.98 us  [per_device(): lax.ppermute(predicted, 'cell', [(dev, dev ^ hop) for dev in range(4)])]
  transfers between devices with their start and end apart: 4 -> 5, of which waited for: 4 -> 5; matrix products, arithmetic and copies ran while one was open for 0% -> 0% of each run, Pallas kernels for 0% -> 0%
where the time goes in v1:
time: 518 us; the launch traced here: 512 us
  other arithmetic  241 us (47%)
  waiting for transfers between devices  152 us (29%)
  local copies, waits for them, and re-layouts  60.7 us (12%)
  matrix products  32 us (6%)
  between operations  18.7 us (4%)
  starting transfers between devices  6.84 us (1%)
    psum x3, waiting for transfers between devices, per_device(): gram_matrix, cross_term = lax.psum((gram_matrix, cross_term), 'obs')  98.7 us
    another operation x21, other arithmetic, per_device(): factor = jnp.linalg.cholesky(gram_matrix + inflation * identity)  88.6 us
    reduce_sum x16, other arithmetic, one_group(): return jnp.sum(picked * group_weight[None], axis=2)  83 us
    another operation x14, other arithmetic, per_device(): member_weight = jax.scipy.linalg.cho_solve((factor, True), cross_term)  59.8 us
    gather x16, local copies, waits for them, and re-layouts, one_group(): picked = jnp.take(blocks, group_index, axis=1)  59.3 us
    ppermute x2, waiting for transfers between devices, per_device(): lax.ppermute(predicted, 'cell', [(dev, dev ^ hop) for dev in range(4)])  53.3 us
    another operation x18, matrix products, per_device(): member_weight = jax.scipy.linalg.cho_solve((factor, True), cross_term)  11.1 us
  transfers between devices with their start and end apart: 5, of which 5 were waited for; matrix products, arithmetic and copies ran while one was open for 0% of the time, Pallas kernels for 0%

profile of v1, /device:TPU:0, one launch (start us, length us, event | category | flops | bytes accessed | tf_op | source)
XLA Modules:
  0.0 512.4 jit_solution(2806110637296299627)
XLA Ops:
  10.8 143.9 %while.14 = (s32[]{:T(128)}, f32[16,200,64]{1,2,0:T(8,128)S(1)}, s32[16,64]{1,0:T(8,128)S(1)}, f32[200,4,128]{2,0,1:T(8,128)S(1)}, f32[16,64,128]{2,1,0:T(8,128)S(1)}, /*index=5*/s32[]{:T(128)}) while((s32[]{:T(128)}, f32[16,200,64]{1,2,0:T(8,128)S(1)}, s32[16,64]{1,0:T(8,128)S(1)}, f32[200,4,128]{2,0,1:T(8,128)S(1)}, ...), condition=%wide.region_2.3_spmd, body=%wide.region_0.2_spmd.sunk | while | flops 4904002 | bytes 19946964 | solution.py:24
  14.6 5.2 %multiply_reduce_fusion.2 = f32[64,200]{1,0:T(8,128)S(1)} fusion(f32[64,200,128]{2,1,0:T(8,128)} %gather_fusion, f32[64,128]{1,0:T(8,128)S(1)} %dynamic-slice_bitcast_fusion.2, pred[64]{0:T(512)(128)(4,1)S(1)} %compare_and_fusion.2), kind=kLoop, calls=%fused_computation.1.clone.1 | loop fusion | flops 4902400 | bytes 6637632 | tf_op jit(solution)/shard_map/while/body/eval_jaxpr/reduce_sum | solution.py:22
  23.6 5.2 %multiply_reduce_fusion.2 = f32[64,200]{1,0:T(8,128)S(1)} fusion(f32[64,200,128]{2,1,0:T(8,128)} %gather_fusion, f32[64,128]{1,0:T(8,128)S(1)} %dynamic-slice_bitcast_fusion.2, pred[64]{0:T(512)(128)(4,1)S(1)} %compare_and_fusion.2), kind=kLoop, calls=%fused_computation.1.clone.1 | loop fusion | flops 4902400 | bytes 6637632 | tf_op jit(solution)/shard_map/while/body/eval_jaxpr/reduce_sum | solution.py:22
  32.6 5.2 %multiply_reduce_fusion.2 = f32[64,200]{1,0:T(8,128)S(1)} fusion(f32[64,200,128]{2,1,0:T(8,128)} %gather_fusion, f32[64,128]{1,0:T(8,128)S(1)} %dynamic-slice_bitcast_fusion.2, pred[64]{0:T(512)(128)(4,1)S(1)} %compare_and_fusion.2), kind=kLoop, calls=%fused_computation.1.clone.1 | loop fusion | flops 4902400 | bytes 6637632 | tf_op jit(solution)/shard_map/while/body/eval_jaxpr/reduce_sum | solution.py:22
  41.6 5.2 %multiply_reduce_fusion.2 = f32[64,200]{1,0:T(8,128)S(1)} fusion(f32[64,200,128]{2,1,0:T(8,128)} %gather_fusion, f32[64,128]{1,0:T(8,128)S(1)} %dynamic-slice_bitcast_fusion.2, pred[64]{0:T(512)(128)(4,1)S(1)} %compare_and_fusion.2), kind=kLoop, calls=%fused_computation.1.clone.1 | loop fusion | flops 4902400 | bytes 6637632 | tf_op jit(solution)/shard_map/while/body/eval_jaxpr/reduce_sum | solution.py:22
  50.6 5.2 %multiply_reduce_fusion.2 = f32[64,200]{1,0:T(8,128)S(1)} fusion(f32[64,200,128]{2,1,0:T(8,128)} %gather_fusion, f32[64,128]{1,0:T(8,128)S(1)} %dynamic-slice_bitcast_fusion.2, pred[64]{0:T(512)(128)(4,1)S(1)} %compare_and_fusion.2), kind=kLoop, calls=%fused_computation.1.clone.1 | loop fusion | flops 4902400 | bytes 6637632 | tf_op jit(solution)/shard_map/while/body/eval_jaxpr/reduce_sum | solution.py:22
  59.5 5.2 %multiply_reduce_fusion.2 = f32[64,200]{1,0:T(8,128)S(1)} fusion(f32[64,200,128]{2,1,0:T(8,128)} %gather_fusion, f32[64,128]{1,0:T(8,128)S(1)} %dynamic-slice_bitcast_fusion.2, pred[64]{0:T(512)(128)(4,1)S(1)} %compare_and_fusion.2), kind=kLoop, calls=%fused_computation.1.clone.1 | loop fusion | flops 4902400 | bytes 6637632 | tf_op jit(solution)/shard_map/while/body/eval_jaxpr/reduce_sum | solution.py:22
  68.5 5.2 %multiply_reduce_fusion.2 = f32[64,200]{1,0:T(8,128)S(1)} fusion(f32[64,200,128]{2,1,0:T(8,128)} %gather_fusion, f32[64,128]{1,0:T(8,128)S(1)} %dynamic-slice_bitcast_fusion.2, pred[64]{0:T(512)(128)(4,1)S(1)} %compare_and_fusion.2), kind=kLoop, calls=%fused_computation.1.clone.1 | loop fusion | flops 4902400 | bytes 6637632 | tf_op jit(solution)/shard_map/while/body/eval_jaxpr/reduce_sum | solution.py:22
  77.5 5.2 %multiply_reduce_fusion.2 = f32[64,200]{1,0:T(8,128)S(1)} fusion(f32[64,200,128]{2,1,0:T(8,128)} %gather_fusion, f32[64,128]{1,0:T(8,128)S(1)} %dynamic-slice_bitcast_fusion.2, pred[64]{0:T(512)(128)(4,1)S(1)} %compare_and_fusion.2), kind=kLoop, calls=%fused_computation.1.clone.1 | loop fusion | flops 4902400 | bytes 6637632 | tf_op jit(solution)/shard_map/while/body/eval_jaxpr/reduce_sum | solution.py:22
  86.5 5.2 %multiply_reduce_fusion.2 = f32[64,200]{1,0:T(8,128)S(1)} fusion(f32[64,200,128]{2,1,0:T(8,128)} %gather_fusion, f32[64,128]{1,0:T(8,128)S(1)} %dynamic-slice_bitcast_fusion.2, pred[64]{0:T(512)(128)(4,1)S(1)} %compare_and_fusion.2), kind=kLoop, calls=%fused_computation.1.clone.1 | loop fusion | flops 4902400 | bytes 6637632 | tf_op jit(solution)/shard_map/while/body/eval_jaxpr/reduce_sum | solution.py:22
  95.5 5.2 %multiply_reduce_fusion.2 = f32[64,200]{1,0:T(8,128)S(1)} fusion(f32[64,200,128]{2,1,0:T(8,128)} %gather_fusion, f32[64,128]{1,0:T(8,128)S(1)} %dynamic-slice_bitcast_fusion.2, pred[64]{0:T(512)(128)(4,1)S(1)} %compare_and_fusion.2), kind=kLoop, calls=%fused_computation.1.clone.1 | loop fusion | flops 4902400 | bytes 6637632 | tf_op jit(solution)/shard_map/while/body/eval_jaxpr/reduce_sum | solution.py:22
  104.5 5.2 %multiply_reduce_fusion.2 = f32[64,200]{1,0:T(8,128)S(1)} fusion(f32[64,200,128]{2,1,0:T(8,128)} %gather_fusion, f32[64,128]{1,0:T(8,128)S(1)} %dynamic-slice_bitcast_fusion.2, pred[64]{0:T(512)(128)(4,1)S(1)} %compare_and_fusion.2), kind=kLoop, calls=%fused_computation.1.clone.1 | loop fusion | flops 4902400 | bytes 6637632 | tf_op jit(solution)/shard_map/while/body/eval_jaxpr/reduce_sum | solution.py:22
  113.5 5.2 %multiply_reduce_fusion.2 = f32[64,200]{1,0:T(8,128)S(1)} fusion(f32[64,200,128]{2,1,0:T(8,128)} %gather_fusion, f32[64,128]{1,0:T(8,128)S(1)} %dynamic-slice_bitcast_fusion.2, pred[64]{0:T(512)(128)(4,1)S(1)} %compare_and_fusion.2), kind=kLoop, calls=%fused_computation.1.clone.1 | loop fusion | flops 4902400 | bytes 6637632 | tf_op jit(solution)/shard_map/while/body/eval_jaxpr/reduce_sum | solution.py:22
  122.5 5.2 %multiply_reduce_fusion.2 = f32[64,200]{1,0:T(8,128)S(1)} fusion(f32[64,200,128]{2,1,0:T(8,128)} %gather_fusion, f32[64,128]{1,0:T(8,128)S(1)} %dynamic-slice_bitcast_fusion.2, pred[64]{0:T(512)(128)(4,1)S(1)} %compare_and_fusion.2), kind=kLoop, calls=%fused_computation.1.clone.1 | loop fusion | flops 4902400 | bytes 6637632 | tf_op jit(solution)/shard_map/while/body/eval_jaxpr/reduce_sum | solution.py:22
  131.5 5.2 %multiply_reduce_fusion.2 = f32[64,200]{1,0:T(8,128)S(1)} fusion(f32[64,200,128]{2,1,0:T(8,128)} %gather_fusion, f32[64,128]{1,0:T(8,128)S(1)} %dynamic-slice_bitcast_fusion.2, pred[64]{0:T(512)(128)(4,1)S(1)} %compare_and_fusion.2), kind=kLoop, calls=%fused_computation.1.clone.1 | loop fusion | flops 4902400 | bytes 6637632 | tf_op jit(solution)/shard_map/while/body/eval_jaxpr/reduce_sum | solution.py:22
  158.2 18.2 %collective-permute-done = f32[200,1024]{1,0:T(8,128)S(1)} collective-permute-done((f32[200,1024]{1,0:T(8,128)S(1)}, f32[200,1024]{1,0:T(8,128)S(1)}, u32[]{:S(2)}, u32[]{:S(2)}) %collective-permute-start) | collective-permute-done | bytes 819232 | tf_op jit(solution)/shard_map/ppermute | solution.py:44
  179.4 35.0 %collective-permute-done.1 = f32[200,1024]{1,0:T(8,128)S(1)} collective-permute-done((f32[200,1024]{1,0:T(8,128)S(1)}, f32[200,1024]{1,0:T(8,128)S(1)}, u32[]{:S(2)}, u32[]{:S(2)}) %collective-permute-start.1) | collective-permute-done | bytes 819232 | tf_op jit(solution)/shard_map/ppermute | solution.py:44
  219.7 33.3 %all-reduce.14.cloned.1.call-done = (f32[200,200]{1,0:T(8,128)}, f32[200,200]{0,1:T(8,128)}) async-done(((f32[200,200]{1,0:T(8,128)}, f32[200,200]{0,1:T(8,128)}), (f32[200,200]{1,0:T(8,128)}, f32[200,200]{0,1:T(8,128)})) %all-reduce.14.cloned.1.call-update) | async-done | bytes 320016 | tf_op jit(solution)/shard_map/psum | solution.py:58
  255.1 11.7 %cholesky.182 = f32[128,128]{1,0:T(8,128)S(1)} custom-call(f32[128,128]{1,0:T(8,128)S(1)} %cholesky.292), custom_call_target="Cholesky" | custom-call | tf_op jit(solution)/shard_map/jit(cholesky)/cholesky | solution.py:59
  266.8 9.8 %custom-call.17 = f32[1,128,128]{1,2,0:T(8,128)S(1)} custom-call(f32[1,128,128]{2,1,0:T(8,128)S(1)} %get-tuple-element.97), custom_call_target="InvertDiagBlocksLowerTriangular" | custom-call | tf_op jit(solution)/shard_map/jit(cholesky)/cholesky | solution.py:59
  277.1 6.6 %cholesky.202 = f32[72,72]{1,0:T(8,128)S(1)} custom-call(f32[72,72]{1,0:T(8,128)S(1)} %convolution_subtract_fusion.8), custom_call_target="Cholesky" | custom-call | tf_op jit(solution)/shard_map/jit(cholesky)/cholesky | solution.py:59
  286.5 19.8 %custom-call.18 = f32[2,128,128]{1,2,0:T(8,128)S(1)} custom-call(f32[2,128,128]{2,1,0:T(8,128)S(1)} %pad_maximum_fusion.9), custom_call_target="InvertDiagBlocksLowerTriangular" | custom-call | tf_op jit(solution)/shard_map/jit(_cho_solve)/triangular_solve | solution.py:60
  316.5 32.8 %all-reduce.12.cloned.1.call-done = (f32[200,200]{1,0:T(8,128)}, f32[200,200]{0,1:T(8,128)}) async-done(((f32[200,200]{1,0:T(8,128)}, f32[200,200]{0,1:T(8,128)}), (f32[200,200]{1,0:T(8,128)}, f32[200,200]{0,1:T(8,128)})) %all-reduce.12.cloned.1.call-update) | async-done | bytes 320016 | tf_op jit(solution)/shard_map/psum | solution.py:58
  351.4 11.7 %cholesky.220 = f32[128,128]{1,0:T(8,128)S(1)} custom-call(f32[128,128]{1,0:T(8,128)S(1)} %cholesky.295), custom_call_target="Cholesky" | custom-call | tf_op jit(solution)/shard_map/jit(cholesky)/cholesky | solution.py:59
  363.2 9.8 %custom-call.19 = f32[1,128,128]{1,2,0:T(8,128)S(1)} custom-call(f32[1,128,128]{2,1,0:T(8,128)S(1)} %get-tuple-element.95), custom_call_target="InvertDiagBlocksLowerTriangular" | custom-call | tf_op jit(solution)/shard_map/jit(cholesky)/cholesky | solution.py:59
  373.4 6.6 %cholesky.240 = f32[72,72]{1,0:T(8,128)S(1)} custom-call(f32[72,72]{1,0:T(8,128)S(1)} %convolution_subtract_fusion.7), custom_call_target="Cholesky" | custom-call | tf_op jit(solution)/shard_map/jit(cholesky)/cholesky | solution.py:59
  382.8 19.9 %custom-call.20 = f32[2,128,128]{1,2,0:T(8,128)S(1)} custom-call(f32[2,128,128]{2,1,0:T(8,128)S(1)} %pad_maximum_fusion.10), custom_call_target="InvertDiagBlocksLowerTriangular" | custom-call | tf_op jit(solution)/shard_map/jit(_cho_solve)/triangular_solve | solution.py:60
  412.6 32.5 %all-reduce.10.cloned.1.call-done = (f32[200,200]{1,0:T(8,128)}, f32[200,200]{0,1:T(8,128)}) async-done(((f32[200,200]{1,0:T(8,128)}, f32[200,200]{0,1:T(8,128)}), (f32[200,200]{1,0:T(8,128)}, f32[200,200]{0,1:T(8,128)})) %all-reduce.10.cloned.1.call-update) | async-done | bytes 320016 | tf_op jit(solution)/shard_map/psum | solution.py:58
  447.2 11.7 %cholesky.258 = f32[128,128]{1,0:T(8,128)S(1)} custom-call(f32[128,128]{1,0:T(8,128)S(1)} %cholesky.298), custom_call_target="Cholesky" | custom-call | tf_op jit(solution)/shard_map/jit(cholesky)/cholesky | solution.py:59
  459.0 9.8 %custom-call.21 = f32[1,128,128]{1,2,0:T(8,128)S(1)} custom-call(f32[1,128,128]{2,1,0:T(8,128)S(1)} %get-tuple-element.93), custom_call_target="InvertDiagBlocksLowerTriangular" | custom-call | tf_op jit(solution)/shard_map/jit(cholesky)/cholesky | solution.py:59
  469.3 6.8 %cholesky.278 = f32[72,72]{1,0:T(8,128)S(1)} custom-call(f32[72,72]{1,0:T(8,128)S(1)} %convolution_subtract_fusion.6), custom_call_target="Cholesky" | custom-call | tf_op jit(solution)/shard_map/jit(cholesky)/cholesky | solution.py:59
  478.9 19.7 %custom-call.22 = f32[2,128,128]{1,2,0:T(8,128)S(1)} custom-call(f32[2,128,128]{2,1,0:T(8,128)S(1)} %pad_maximum_fusion.11), custom_call_target="InvertDiagBlocksLowerTriangular" | custom-call | tf_op jit(solution)/shard_map/jit(_cho_solve)/triangular_solve | solution.py:60
  (211 shorter events, 124.3 us)
Async XLA Ops:
  7.2 245.9 %all-reduce.14.cloned.1.call-start = ((), (), s32[]{:S(2)}) async-start(), calls=%async_computation.2 | async-start | bytes 819200 | tf_op jit(solution)/shard_map/psum | solution.py:58
  10.8 168.6 %copy-start = (bf16[200,512]{1,0:T(8,128)(2,1)S(1)}, bf16[200,512]{1,0:T(8,128)(2,1)}, u32[]{:S(2)}) copy-start(bf16[200,512]{1,0:T(8,128)(2,1)} %param.11) | copy-start | bytes 614404
  10.8 168.6 %copy-start.1 = (f32[1024]{0:T(1024)S(1)}, f32[1024]{0:T(1024)}, u32[]{:S(2)}) copy-start(f32[1024]{0:T(1024)} %param.15) | copy-start | bytes 12292
  154.7 61.5 %copy-start.2 = (f32[1024]{0:T(1024)S(1)}, f32[1024]{0:T(1024)}, u32[]{:S(2)}) copy-start(f32[1024]{0:T(1024)} %param.14) | copy-start | bytes 12292
  155.0 21.4 %collective-permute-start = (f32[200,1024]{1,0:T(8,128)S(1)}, f32[200,1024]{1,0:T(8,128)S(1)}, u32[]{:S(2)}, u32[]{:S(2)}) collective-permute-start(f32[200,1024]{1,0:T(8,128)S(1)} %copy.33), channel_id=1, source_target_pairs={{0,4},{4,0},{8,12},{12,8},{1,5},{5,1},{9,13},{13,9},{2,6},{6,2},{1... | collective-permute-start | bytes 2457608 | tf_op jit(solution)/shard_map/ppermute | solution.py:44
  176.5 37.9 %collective-permute-start.1 = (f32[200,1024]{1,0:T(8,128)S(1)}, f32[200,1024]{1,0:T(8,128)S(1)}, u32[]{:S(2)}, u32[]{:S(2)}) collective-permute-start(f32[200,1024]{1,0:T(8,128)S(1)} %add.126), channel_id=1, source_target_pairs={{0,8},{4,12},{8,0},{12,4},{1,9},{5,13},{9,1},{13,5},{2,10},{6,14},... | collective-permute-start | bytes 2457608 | tf_op jit(solution)/shard_map/ppermute | solution.py:44
  219.1 130.2 %all-reduce.12.cloned.1.call-start = ((), (), s32[]{:S(2)}) async-start(), calls=%async_computation.1 | async-start | bytes 819200 | tf_op jit(solution)/shard_map/psum | solution.py:58
  316.2 128.9 %all-reduce.10.cloned.1.call-start = ((), (), s32[]{:S(2)}) async-start(), calls=%async_computation | async-start | bytes 819200 | tf_op jit(solution)/shard_map/psum | solution.py:58
Sparse Core Ops, SparseCore 0:
  219.3 33.7 all-reduce.13
  316.4 32.9 all-reduce.11
  412.2 32.9 all-reduce.9
